TPU v7x, 32 devices: a whole 2x2x4 slice. The times are simulated.
32 devices in a mesh: groups: 2 (over y), ep: 4 (over z), dp: 4 (over x, core), tp: 1.
Axes of the slice: x: 2, y: 2, z: 4, core: 2. Of those that a mesh axis runs over, the one named last changes fastest.
Arguments:
- tokens: bfloat16 [2048, 2048], P(('groups', 'ep', 'dp', 'tp')), parts along dimension 0, may hold values from -6 to 6
- experts_one: int32 [2048, 8], P(('groups', 'ep', 'dp', 'tp')), parts along dimension 0, may hold values from 0 to 15, all different within a row; in each aligned block of 64 rows (0 to 63, 64 to 127, ...) at most 40 rows name the same one
- gates_one: float32 [2048, 8], P(('groups', 'ep', 'dp', 'tp')), parts along dimension 0, may hold values from 0.05 to 0.5
- w_in_one: bfloat16 [16, 2048, 2, 768], P(('ep', 'dp'), None, None, 'tp'), may hold values from -0.125 to 0.125
- w_down_one: bfloat16 [16, 768, 2048], P(('ep', 'dp'), 'tp'), may hold values from -0.21875 to 0.21875
- norm_gain: float32 [2048], replicated, may hold values from 0.5 to 1.5
- experts_two: int32 [2048, 8], P(('groups', 'ep', 'dp', 'tp')), parts along dimension 0, may hold values from 0 to 15, all different within a row; in each aligned block of 64 rows (0 to 63, 64 to 127, ...) at most 40 rows name the same one
- gates_two: float32 [2048, 8], P(('groups', 'ep', 'dp', 'tp')), parts along dimension 0, may hold values from 0.05 to 0.5
- placement_two: int32 [16], replicated, may hold values from 0 to 15, each once
- w_in_two: bfloat16 [16, 2048, 2, 768], P(('ep', 'dp'), None, None, 'tp'), may hold values from -0.125 to 0.125
- w_down_two: bfloat16 [16, 768, 2048], P(('ep', 'dp'), 'tp'), may hold values from -0.21875 to 0.21875
Outputs:
- layer_out: bfloat16 [2048, 2048], P(('groups', 'ep', 'dp', 'tp')), parts along dimension 0
There are 2 independent parts, one for each index of `groups`. A program takes and returns all parts, laid end to end along the dimension named above; an argument that names none is the same for every part. Nothing has to cross between parts.
Inputs may be any that keep to these rules, and one draw needn't show every extreme that they name: `experts_one`: each token names 8 different experts; among the 64 tokens of one device no expert is named more than 40 times, and on some device some expert is named exactly 40 times. `experts_two`: each token names 8 different experts; among the 64 tokens of one device no expert is named more than 40 times, and on some device some expert is named exactly 40 times. `placement_two`: each slot is named by exactly one expert.
All inputs are finite; a program needn't handle non-finite values.
Results may differ from a plain program's by a relative error of at most 0.011.
Values may be sent and summed in bfloat16 or wider, within the bound.
No kernel may reach another device: no remote copies, remote signals or barrier semaphores. Data moves between devices by JAX's collectives and lax.ppermute only.
A program may use at most 128 MiB of HBM per device.

v0:
```python
import jax
import jax.numpy as jnp
from jax import lax
from jax.sharding import PartitionSpec as P


def capacity(tok_rows, top_count, expert_count):
    return max(2, min(tok_rows, 5 * tok_rows * top_count // (4 * expert_count)))


def pack_rows(rows_in, targets, expert_count, per_slot):
    tok_rows, top_count = targets.shape
    flat_ids = targets.reshape(-1)
    hit_table = (flat_ids[:, None] == jnp.arange(expert_count, dtype=jnp.int32)[None, :]).astype(
        jnp.int32
    )
    before = jnp.cumsum(hit_table, axis=0) - hit_table
    slot_rank = jnp.sum(before * hit_table, axis=1)
    slot_index = flat_ids * per_slot + slot_rank
    source = jnp.arange(tok_rows * top_count, dtype=jnp.int32) // top_count
    owner_row = jnp.zeros((expert_count * per_slot,), jnp.int32).at[slot_index].set(source)
    filled = jnp.zeros((expert_count * per_slot,), jnp.int32).at[slot_index].set(1)
    buffer = jnp.where(filled[:, None] > 0, rows_in[owner_row], jnp.zeros((), rows_in.dtype))
    return (buffer, slot_index)


def to_experts(buffer, expert_count, per_slot):
    row_width = buffer.shape[1]
    arrived = lax.all_to_all(
        buffer.reshape(expert_count, per_slot, row_width),
        ("ep", "dp"),
        split_axis=0,
        concat_axis=0,
        tiled=True,
    )
    return arrived.reshape(expert_count * per_slot, row_width)


def to_owners(produced, expert_count, per_slot):
    row_width = produced.shape[1]
    returned = lax.all_to_all(
        produced.reshape(expert_count, per_slot, row_width),
        ("ep", "dp"),
        split_axis=0,
        concat_axis=0,
        tiled=True,
    )
    return returned.reshape(expert_count * per_slot, row_width)


def run_expert(received, w_in, w_down):
    row_width = received.shape[1]
    down_local = w_down[0]
    half_width = down_local.shape[0]
    w_local = w_in.reshape(row_width, 2 * half_width)
    gate_up = jnp.dot(
        lax.all_gather(received, "tp", axis=0, tiled=True),
        w_local,
        preferred_element_type=jnp.float32,
    )
    hidden = (jax.nn.silu(gate_up[:, :half_width]) * gate_up[:, half_width:]).astype(jnp.bfloat16)
    return lax.psum_scatter(
        jnp.dot(hidden, down_local, preferred_element_type=jnp.float32).astype(jnp.bfloat16),
        "tp",
        scatter_dimension=0,
        tiled=True,
    )


def moe_block(rows_in, targets, gate_values, w_in, w_down, expert_count, per_slot):
    tok_rows, top_count = targets.shape
    row_width = rows_in.shape[1]
    buffer, slot_index = pack_rows(rows_in, targets, expert_count, per_slot)
    arrived = to_experts(buffer, expert_count, per_slot)
    produced = run_expert(arrived, w_in, w_down)
    returned = to_owners(produced, expert_count, per_slot)
    picked = returned[slot_index].reshape(tok_rows, top_count, row_width)
    return jnp.sum(gate_values[:, :, None] * picked.astype(jnp.float32), axis=1)


def shards(
    tokens,
    experts_one,
    gates_one,
    w_in_one,
    w_down_one,
    norm_gain,
    experts_two,
    gates_two,
    placement_two,
    w_in_two,
    w_down_two,
):
    tok_rows, top_count = experts_one.shape
    expert_count = placement_two.shape[0]
    per_slot = capacity(tok_rows, top_count, expert_count)
    moe_one = moe_block(
        tokens, experts_one, gates_one, w_in_one, w_down_one, expert_count, per_slot
    )
    mixed = (tokens.astype(jnp.float32) + moe_one).astype(jnp.bfloat16)
    mixed = lax.optimization_barrier(mixed)
    mixed_wide = mixed.astype(jnp.float32)
    inv_rms = lax.rsqrt(jnp.mean(mixed_wide * mixed_wide, axis=1, keepdims=True) + 1e-06)
    normed = (mixed_wide * inv_rms * norm_gain[None, :]).astype(jnp.bfloat16)
    expert_range = jnp.arange(expert_count, dtype=jnp.int32)
    matches = experts_two[:, :, None] == expert_range[None, None, :]
    layer_slots = jnp.sum(jnp.where(matches, placement_two[None, None, :], 0), axis=2)
    moe_two = moe_block(
        normed, layer_slots, gates_two, w_in_two, w_down_two, expert_count, per_slot
    )
    return (mixed_wide + moe_two).astype(jnp.bfloat16)


def solution(mesh):
    in_specs = (
        P(("groups", "ep", "dp", "tp"), None),
        P(("groups", "ep", "dp", "tp"), None),
        P(("groups", "ep", "dp", "tp"), None),
        P(("ep", "dp"), None, None, "tp"),
        P(("ep", "dp"), "tp", None),
        P(),
        P(("groups", "ep", "dp", "tp"), None),
        P(("groups", "ep", "dp", "tp"), None),
        P(),
        P(("ep", "dp"), None, None, "tp"),
        P(("ep", "dp"), "tp", None),
    )
    out_specs = P(("groups", "ep", "dp", "tp"), None)
    return jax.shard_map(shards, mesh=mesh, in_specs=in_specs, out_specs=out_specs, check_vma=False)
```

profile of v0, /device:TPU:11, one launch (start us, length us, event | category | flops | bytes accessed | tf_op | source)
XLA Modules:
  0.0 317.4 jit_solution(6289434253920874725)
XLA Ops:
  0.0 0.0 copy-start
  0.0 0.9 copy.28
  0.9 0.1 eq.67
  1.0 0.1 eq.63
  1.1 0.7 broadcast_multiply_fusion.1
  1.8 1.2 reduce-window.14
  3.0 0.2 slice_reduce_fusion.1
  3.2 0.1 copy.27
  3.3 0.1 mul.82
  3.4 0.1 fusion.19
  3.5 2.4 scatter_custom_fusion.1
  6.0 2.4 scatter_custom_fusion
  8.5 0.1 broadcast_in_dim.57
  8.6 0.0 copy-done.2
  8.6 4.1 %gather_fusion = bf16[640,2048]{1,0:T(8,128)(2,1)} fusion(bf16[64,2048]{1,0:T(8,128)(2,1)S(1)} %copy-done.2, s32[1024]{0:T(1024)S(1)} %pad_clamp_fusion.3), kind=kCustom, calls=%fused_computation | custom fusion | bytes 5245440 | tf_op jit(solution)/shard_map/gather | solution.py:23
  12.7 3.5 %broadcast_select_fusion.1 = bf16[16,40,2048]{2,1,0:T(8,128)(2,1)} fusion(bf16[16,40,2048]{2,1,0:T(8,128)(2,1)} %bitcast.74, pred[16,40]{1,0:T(8,128)(4,1)S(1)} %broadcast_in_dim.57), kind=kLoop, calls=%fused_computation.17 | loop fusion | flops 1310720 | bytes 5243520 | tf_op jit(solution)/shard_map/jit(_where)/select_n | solution.py:23
  16.2 6.5 %all-to-all-start = ((bf16[16,40,2048]{2,1,0:T(8,128)(2,1)}), bf16[16,40,2048]{2,1,0:T(8,128)(2,1)}, u32[]{:S(2)}, u32[]{:S(2)}) async-start(bf16[16,40,2048]{2,1,0:T(8,128)(2,1)} %broadcast_select_fusion.1), calls=%async_computation | async-start | bytes 5242880 | tf_op jit(solution)/shard_map/all_to_all | solution.py:29
  22.7 6.8 %copy.38 = bf16[256,8,2,768]{3,1,2,0:T(8,128)(2,1)} copy(bf16[256,8,2,768]{3,2,1,0:T(2,128)(2,1)} %bitcast.75) | data formatting | bytes 12582912
  29.5 52.0 %all-to-all-done = bf16[16,40,2048]{2,1,0:T(8,128)(2,1)} async-done(((bf16[16,40,2048]{2,1,0:T(8,128)(2,1)}), bf16[16,40,2048]{2,1,0:T(8,128)(2,1)}, u32[]{:S(2)}, u32[]{:S(2)}) %all-to-all-start) | async-done | bytes 2621472 | tf_op jit(solution)/shard_map/all_to_all | solution.py:29
  81.5 7.1 %fusion.35 = f32[640,1536]{1,0:T(8,128)S(1)} fusion(bf16[640,2048]{1,0:T(8,128)(2,1)} %bitcast.4, bf16[2048,1536]{1,0:T(8,128)(2,1)} %bitcast.77), kind=kOutput, calls=%fused_computation.82 | convolution fusion | flops 4026531840 | bytes 12845056 | tf_op jit(solution)/shard_map/dot_general | solution.py:56
  88.6 0.0 copy-done
  88.6 3.8 %convolution_convert_fusion.1 = bf16[640,2048]{1,0:T(8,128)(2,1)} fusion(bf16[1,768,2048]{2,1,0:T(8,128)(2,1)S(1)} %copy-done, f32[640,1536]{1,0:T(8,128)S(1)} %fusion.35), kind=kOutput, calls=%fused_computation.13 | convolution fusion | flops 2017525760 | bytes 9699328 | tf_op jit(solution)/shard_map/dot_general | solution.py:63
  92.4 4.9 %all-to-all-start.1 = ((bf16[16,40,2048]{2,1,0:T(8,128)(2,1)}), bf16[16,40,2048]{2,1,0:T(8,128)(2,1)S(1)}, u32[]{:S(2)}, u32[]{:S(2)}) async-start(bf16[16,40,2048]{2,1,0:T(8,128)(2,1)} %bitcast.79), calls=%async_computation.1 | async-start | bytes 5242880 | tf_op jit(solution)/shard_map/all_to_all | solution.py:41
  97.3 0.0 copy-done.8
  97.3 0.0 copy-done.9
  97.3 0.1 select_reduce_fusion
  97.4 0.1 copy.33
  97.5 0.1 eq.78
  97.6 0.1 eq.74
  97.7 1.2 reduce-window.16
  98.8 0.2 slice_reduce_fusion
  99.1 0.1 copy.32
  99.2 0.1 mul.89
  99.3 0.1 fusion.16
  99.4 2.4 scatter_custom_fusion.3
  101.8 2.6 scatter_custom_fusion.2
  104.5 0.0 copy-done.6
  104.5 0.1 copy.26
  104.6 0.1 broadcast_in_dim.63
  104.7 51.2 %all-to-all-done.1 = bf16[16,40,2048]{2,1,0:T(8,128)(2,1)S(1)} async-done(((bf16[16,40,2048]{2,1,0:T(8,128)(2,1)}), bf16[16,40,2048]{2,1,0:T(8,128)(2,1)S(1)}, u32[]{:S(2)}, u32[]{:S(2)}) %all-to-all-start.1) | async-done | bytes 2621472 | tf_op jit(solution)/shard_map/all_to_all | solution.py:41
  155.9 3.3 %gather_fusion.1 = bf16[512,2048]{1,0:T(8,128)(2,1)} fusion(bf16[640,2048]{1,0:T(8,128)(2,1)S(1)} %bitcast.72, s32[1024]{0:T(1024)S(1)} %pad_clamp_fusion.2), kind=kCustom, calls=%fused_computation.1 | custom fusion | bytes 4196352 | tf_op jit(solution)/shard_map/gather | solution.py:77
  159.3 3.4 %fusion.1 = f32[64,2048]{1,0:T(8,128)S(1)} fusion(bf16[512,2048]{1,0:T(8,128)(2,1)} %gather_fusion.1, f32[64,8]{1,0:T(8,128)S(1)} %copy.26), kind=kLoop, calls=%fused_computation.11 | loop fusion | flops 3014656 | bytes 2623488 | tf_op jit(solution)/shard_map/reduce_sum | solution.py:78
  162.8 0.0 copy-start.3
  162.8 0.2 fusion.10
  162.9 0.0 copy-done.5
  162.9 0.1 fusion.12
  163.1 3.4 %gather_fusion.2 = bf16[640,2048]{1,0:T(8,128)(2,1)S(1)} fusion(bf16[64,2048]{1,0:T(8,128)(2,1)S(1)} %fusion.12, s32[1024]{0:T(1024)S(1)} %pad_clamp_fusion.1), kind=kCustom, calls=%fused_computation.2 | custom fusion | bytes 5245440 | tf_op jit(solution)/shard_map/gather | solution.py:23
  166.5 0.0 copy-done.3
  166.5 1.8 broadcast_select_fusion
  168.3 4.8 %all-to-all-start.2 = ((bf16[16,40,2048]{2,1,0:T(8,128)(2,1)}), bf16[16,40,2048]{2,1,0:T(8,128)(2,1)S(1)}, u32[]{:S(2)}, u32[]{:S(2)}) async-start(bf16[16,40,2048]{2,1,0:T(8,128)(2,1)} %broadcast_select_fusion), calls=%async_computation.2 | async-start | bytes 5242880 | tf_op jit(solution)/shard_map/all_to_all | solution.py:29
  173.1 6.8 %copy.39 = bf16[256,8,2,768]{3,1,2,0:T(8,128)(2,1)} copy(bf16[256,8,2,768]{3,2,1,0:T(2,128)(2,1)} %bitcast.76) | data formatting | bytes 12582912
  179.9 51.9 %all-to-all-done.2 = bf16[16,40,2048]{2,1,0:T(8,128)(2,1)S(1)} async-done(((bf16[16,40,2048]{2,1,0:T(8,128)(2,1)}), bf16[16,40,2048]{2,1,0:T(8,128)(2,1)S(1)}, u32[]{:S(2)}, u32[]{:S(2)}) %all-to-all-start.2) | async-done | bytes 2621472 | tf_op jit(solution)/shard_map/all_to_all | solution.py:29
  231.8 6.5 %fusion.36 = f32[640,1536]{1,0:T(8,128)S(1)} fusion(bf16[640,2048]{1,0:T(8,128)(2,1)S(1)} %bitcast.80, bf16[2048,1536]{1,0:T(8,128)(2,1)} %bitcast.78), kind=kOutput, calls=%fused_computation.83 | convolution fusion | flops 4026531840 | bytes 12845056 | tf_op jit(solution)/shard_map/dot_general | solution.py:56
  238.2 0.0 copy-done.10
  238.2 3.8 %convolution_convert_fusion = bf16[640,2048]{1,0:T(8,128)(2,1)} fusion(bf16[1,768,2048]{2,1,0:T(8,128)(2,1)S(1)} %copy-done.10, f32[640,1536]{1,0:T(8,128)S(1)} %fusion.36), kind=kOutput, calls=%fused_computation.12 | convolution fusion | flops 2017525760 | bytes 9699328 | tf_op jit(solution)/shard_map/dot_general | solution.py:63
  242.0 4.9 %all-to-all-start.3 = ((bf16[16,40,2048]{2,1,0:T(8,128)(2,1)}), bf16[16,40,2048]{2,1,0:T(8,128)(2,1)}, u32[]{:S(2)}, u32[]{:S(2)}) async-start(bf16[16,40,2048]{2,1,0:T(8,128)(2,1)} %bitcast.15), calls=%async_computation.3 | async-start | bytes 5242880 | tf_op jit(solution)/shard_map/all_to_all | solution.py:41
  246.9 0.0 copy-done.7
  246.9 0.1 copy.31
  247.0 58.7 %all-to-all-done.3 = bf16[16,40,2048]{2,1,0:T(8,128)(2,1)} async-done(((bf16[16,40,2048]{2,1,0:T(8,128)(2,1)}), bf16[16,40,2048]{2,1,0:T(8,128)(2,1)}, u32[]{:S(2)}, u32[]{:S(2)}) %all-to-all-start.3) | async-done | bytes 2621472 | tf_op jit(solution)/shard_map/all_to_all | solution.py:41
  305.7 7.4 %gather_fusion.3 = bf16[512,2048]{1,0:T(8,128)(2,1)} fusion(bf16[640,2048]{1,0:T(8,128)(2,1)} %bitcast.16, s32[1024]{0:T(1024)S(1)} %pad_clamp_fusion), kind=kCustom, calls=%fused_computation.3 | custom fusion | bytes 4196352 | tf_op jit(solution)/shard_map/gather | solution.py:77
  313.1 3.5 %fusion = f32[64,2048]{1,0:T(8,128)S(1)} fusion(bf16[512,2048]{1,0:T(8,128)(2,1)} %gather_fusion.3, f32[64,8]{1,0:T(8,128)S(1)} %copy.31), kind=kLoop, calls=%fused_computation.9 | loop fusion | flops 3014656 | bytes 2623488 | tf_op jit(solution)/shard_map/reduce_sum | solution.py:78
  316.6 0.0 copy-done.4
  316.6 0.8 fusion.13
  317.4 0.0 copy-done.1
  (30 shorter events, 0.2 us)
Async XLA Ops:
  0.0 88.6 %copy-start = (bf16[1,768,2048]{2,1,0:T(8,128)(2,1)S(1)}, bf16[1,768,2048]{2,1,0:T(8,128)(2,1)}, u32[]{:S(2)}) copy-start(bf16[1,768,2048]{2,1,0:T(8,128)(2,1)} %param.15) | copy-start | bytes 9437188
  0.0 8.6 %copy-start.2 = (bf16[64,2048]{1,0:T(8,128)(2,1)S(1)}, bf16[64,2048]{1,0:T(8,128)(2,1)}, u32[]{:S(2)}) copy-start(bf16[64,2048]{1,0:T(8,128)(2,1)} %param.11) | copy-start | bytes 786436
  16.2 65.3 %all-to-all-start = ((bf16[16,40,2048]{2,1,0:T(8,128)(2,1)}), bf16[16,40,2048]{2,1,0:T(8,128)(2,1)}, u32[]{:S(2)}, u32[]{:S(2)}) async-start(bf16[16,40,2048]{2,1,0:T(8,128)(2,1)} %broadcast_select_fusion.1), calls=%async_computation | async-start | bytes 5242880 | tf_op jit(solution)/shard_map/all_to_all | solution.py:29
  92.4 4.9 %copy-start.8 = (s32[64,8]{0,1:T(8,128)S(1)}, s32[64,8]{0,1:T(8,128)}, u32[]{:S(2)}) copy-start(s32[64,8]{0,1:T(8,128)} %param.17) | copy-start | bytes 6148
  92.4 4.9 %copy-start.9 = (s32[16]{0:T(128)S(1)}, s32[16]{0:T(128)}, u32[]{:S(2)}) copy-start(s32[16]{0:T(128)} %param.19) | copy-start | bytes 196
  92.4 12.1 %copy-start.6 = (f32[64,8]{0,1:T(8,128)S(1)}, f32[64,8]{0,1:T(8,128)}, u32[]{:S(2)}) copy-start(f32[64,8]{0,1:T(8,128)} %param.13) | copy-start | bytes 6148
  92.4 63.6 %all-to-all-start.1 = ((bf16[16,40,2048]{2,1,0:T(8,128)(2,1)}), bf16[16,40,2048]{2,1,0:T(8,128)(2,1)S(1)}, u32[]{:S(2)}, u32[]{:S(2)}) async-start(bf16[16,40,2048]{2,1,0:T(8,128)(2,1)} %bitcast.79), calls=%async_computation.1 | async-start | bytes 5242880 | tf_op jit(solution)/shard_map/all_to_all | solution.py:41
  159.3 3.7 %copy-start.5 = (f32[2048]{0:T(1024)S(1)}, f32[2048]{0:T(1024)}, u32[]{:S(2)}) copy-start(f32[2048]{0:T(1024)} %param.16) | copy-start | bytes 24580
  162.8 3.8 %copy-start.3 = (bf16[64,2048]{1,0:T(8,128)(2,1)}, bf16[64,2048]{1,0:T(8,128)(2,1)S(1)}, u32[]{:S(2)}) copy-start(bf16[64,2048]{1,0:T(8,128)(2,1)S(1)} %add_convert_fusion) | copy-start | bytes 786436
  168.3 63.4 %all-to-all-start.2 = ((bf16[16,40,2048]{2,1,0:T(8,128)(2,1)}), bf16[16,40,2048]{2,1,0:T(8,128)(2,1)S(1)}, u32[]{:S(2)}, u32[]{:S(2)}) async-start(bf16[16,40,2048]{2,1,0:T(8,128)(2,1)} %broadcast_select_fusion), calls=%async_computation.2 | async-start | bytes 5242880 | tf_op jit(solution)/shard_map/all_to_all | solution.py:29
  231.8 6.5 %copy-start.10 = (bf16[1,768,2048]{2,1,0:T(8,128)(2,1)S(1)}, bf16[1,768,2048]{2,1,0:T(8,128)(2,1)}, u32[]{:S(2)}) copy-start(bf16[1,768,2048]{2,1,0:T(8,128)(2,1)} %param.21) | copy-start | bytes 9437188
  242.0 4.9 %copy-start.7 = (f32[64,8]{0,1:T(8,128)S(1)}, f32[64,8]{0,1:T(8,128)}, u32[]{:S(2)}) copy-start(f32[64,8]{0,1:T(8,128)} %param.18) | copy-start | bytes 6148
  242.0 63.7 %all-to-all-start.3 = ((bf16[16,40,2048]{2,1,0:T(8,128)(2,1)}), bf16[16,40,2048]{2,1,0:T(8,128)(2,1)}, u32[]{:S(2)}, u32[]{:S(2)}) async-start(bf16[16,40,2048]{2,1,0:T(8,128)(2,1)} %bitcast.15), calls=%async_computation.3 | async-start | bytes 5242880 | tf_op jit(solution)/shard_map/all_to_all | solution.py:41
  305.7 11.7 %copy-start.1 = (bf16[1,768,2048]{2,1,0:T(8,128)(2,1)S(1)}, bf16[1,768,2048]{2,1,0:T(8,128)(2,1)}, u32[]{:S(2)}) copy-start(bf16[1,768,2048]{2,1,0:T(8,128)(2,1)} %param.15) | copy-start | bytes 9437188
  313.1 3.5 %copy-start.4 = (bf16[64,2048]{1,0:T(8,128)(2,1)S(1)}, bf16[64,2048]{1,0:T(8,128)(2,1)}, u32[]{:S(2)}) copy-start(bf16[64,2048]{1,0:T(8,128)(2,1)} %copy-done.3) | copy-start | bytes 786436
where the time goes:
time: 318 us; the launch traced here: 317 us
  waiting for transfers between devices  214 us (67%)
  local copies, waits for them, and re-layouts  44.4 us (14%)
  starting transfers between devices  21.1 us (7%)
  matrix products  21.1 us (7%)
  other arithmetic  16.7 us (5%)
    all_to_all x2, waiting for transfers between devices, to_owners(): lax.all_to_all(produced.reshape(expert_count, per_slot, row_width), ('ep'...  110 us
    all_to_all x2, waiting for transfers between devices, to_experts(): lax.all_to_all(buffer.reshape(expert_count, per_slot, row_width), ('ep',...  104 us
    unnamed x27, local copies, waits for them, and re-layouts  14.7 us
    dot_general x2, matrix products, run_expert(): jnp.dot(lax.all_gather(received, 'tp', axis=0, tiled=True), w_local, pref...  13.6 us
    all_to_all x2, starting transfers between devices, to_experts(): lax.all_to_all(buffer.reshape(expert_count, per_slot, row_width), ('ep',...  11.3 us
    gather x2, local copies, waits for them, and re-layouts, moe_block(): picked = returned[slot_index].reshape(tok_rows, top_count, row_width)  10.8 us
    all_to_all x2, starting transfers between devices, to_owners(): lax.all_to_all(produced.reshape(expert_count, per_slot, row_width), ('ep'...  9.81 us
    dot_general x2, matrix products, run_expert(): jnp.dot(hidden, down_local, preferred_element_type=jnp.float32)  7.54 us
  transfers between devices with their start and end apart: 4, of which 4 were waited for; matrix products, arithmetic and copies ran while one was open for 7% of the time, Pallas kernels for 0%

commit v1 on v0

--- a/solution.py
+++ b/solution.py
@@ -1,7 +1,13 @@
+import functools
+
 import jax
 import jax.numpy as jnp
 from jax import lax
+from jax.experimental import pallas as pl
+from jax.experimental.pallas import tpu as pltpu
 from jax.sharding import PartitionSpec as P
+
+LANES = 128
 
 
 def capacity(tok_rows, top_count, expert_count):
@@ -24,28 +30,16 @@
     return (buffer, slot_index)
 
 
-def to_experts(buffer, expert_count, per_slot):
+def exchange(buffer, expert_count, per_slot):
     row_width = buffer.shape[1]
-    arrived = lax.all_to_all(
+    moved = lax.all_to_all(
         buffer.reshape(expert_count, per_slot, row_width),
         ("ep", "dp"),
         split_axis=0,
         concat_axis=0,
         tiled=True,
     )
-    return arrived.reshape(expert_count * per_slot, row_width)
-
-
-def to_owners(produced, expert_count, per_slot):
-    row_width = produced.shape[1]
-    returned = lax.all_to_all(
-        produced.reshape(expert_count, per_slot, row_width),
-        ("ep", "dp"),
-        split_axis=0,
-        concat_axis=0,
-        tiled=True,
-    )
-    return returned.reshape(expert_count * per_slot, row_width)
+    return moved.reshape(expert_count * per_slot, row_width)
 
 
 def run_expert(received, w_in, w_down):
@@ -71,14 +65,26 @@
     tok_rows, top_count = targets.shape
     row_width = rows_in.shape[1]
     buffer, slot_index = pack_rows(rows_in, targets, expert_count, per_slot)
-    arrived = to_experts(buffer, expert_count, per_slot)
+    arrived = exchange(buffer, expert_count, per_slot)
     produced = run_expert(arrived, w_in, w_down)
-    returned = to_owners(produced, expert_count, per_slot)
+    returned = exchange(produced, expert_count, per_slot)
     picked = returned[slot_index].reshape(tok_rows, top_count, row_width)
     return jnp.sum(gate_values[:, :, None] * picked.astype(jnp.float32), axis=1)
 
 
-def shards(
+def slots_of(experts_two, placement_two):
+    expert_range = jnp.arange(placement_two.shape[0], dtype=jnp.int32)
+    matches = experts_two[:, :, None] == expert_range[None, None, :]
+    return jnp.sum(jnp.where(matches, placement_two[None, None, :], 0), axis=2)
+
+
+def norm_rows(mixed, norm_gain):
+    mixed_wide = mixed.astype(jnp.float32)
+    inv_rms = lax.rsqrt(jnp.mean(mixed_wide * mixed_wide, axis=1, keepdims=True) + 1e-06)
+    return (mixed_wide * inv_rms * norm_gain[None, :]).astype(jnp.bfloat16)
+
+
+def routed_shards(
     tokens,
     experts_one,
     gates_one,
@@ -99,16 +105,243 @@
     )
     mixed = (tokens.astype(jnp.float32) + moe_one).astype(jnp.bfloat16)
     mixed = lax.optimization_barrier(mixed)
-    mixed_wide = mixed.astype(jnp.float32)
-    inv_rms = lax.rsqrt(jnp.mean(mixed_wide * mixed_wide, axis=1, keepdims=True) + 1e-06)
-    normed = (mixed_wide * inv_rms * norm_gain[None, :]).astype(jnp.bfloat16)
-    expert_range = jnp.arange(expert_count, dtype=jnp.int32)
-    matches = experts_two[:, :, None] == expert_range[None, None, :]
-    layer_slots = jnp.sum(jnp.where(matches, placement_two[None, None, :], 0), axis=2)
+    normed = norm_rows(mixed, norm_gain)
+    layer_slots = slots_of(experts_two, placement_two)
     moe_two = moe_block(
         normed, layer_slots, gates_two, w_in_two, w_down_two, expert_count, per_slot
     )
-    return (mixed_wide + moe_two).astype(jnp.bfloat16)
+    return (mixed.astype(jnp.float32) + moe_two).astype(jnp.bfloat16)
+
+
+def gate_columns(targets, gate_values, expert_count):
+    hits = targets[:, :, None] == jnp.arange(expert_count, dtype=jnp.int32)[None, None, :]
+    table = jnp.sum(jnp.where(hits, gate_values[:, :, None], 0.0), axis=1)
+    high = lax.reduce_precision(table, 8, 7)
+    rest = table - high
+    middle = lax.reduce_precision(rest, 8, 7)
+    low = rest - middle
+    return jnp.concatenate([high, middle, low], axis=1).astype(jnp.bfloat16)
+
+
+def mlp_kernel(block_count, rows, width, half, lane_base, expert_count, chunk, *refs):
+    ids = refs[0]
+    x_in = refs[1 : 1 + block_count]
+    g_in = refs[1 + block_count : 1 + 2 * block_count]
+    weights = refs[1 + 2 * block_count : 5 + 2 * block_count]
+    outs = refs[5 + 2 * block_count : 5 + 3 * block_count]
+    xs, gs, w_in, w_down, hidden, total, x_sem, g_sem, in_sem, down_sem = refs[
+        5 + 3 * block_count :
+    ]
+    pieces = half // chunk
+
+    x_copies, g_copies = [], []
+    for k in range(block_count):
+        span = pl.ds(k * rows, rows)
+        x_copies.append(
+            pltpu.make_async_copy(x_in[k].at[:, pl.ds(0, width)], xs.at[span, :], x_sem.at[k])
+        )
+        g_copies.append(
+            pltpu.make_async_copy(
+                g_in[k].at[:, pl.ds(width, LANES)], gs.at[span, :], g_sem.at[k]
+            )
+        )
+    for copy in x_copies:
+        copy.start()
+    in_copies, down_copies = {}, {}
+    for e in range(2):
+        for j in range(pieces):
+            for part in range(2):
+                cols = pl.ds(part * half + j * chunk, chunk)
+                copy = pltpu.make_async_copy(
+                    weights[2 * e].at[:, cols],
+                    w_in.at[e, part, j],
+                    in_sem.at[e, part, j],
+                )
+                copy.start()
+                in_copies[e, part, j] = copy
+        down_copies[e] = pltpu.make_async_copy(weights[2 * e + 1], w_down.at[e], down_sem.at[e])
+        down_copies[e].start()
+        if e == 0:
+            for copy in g_copies:
+                copy.start()
+    for copy in x_copies:
+        copy.wait()
+    for e in range(2):
+        for j in range(pieces):
+            in_copies[e, 0, j].wait()
+            in_copies[e, 1, j].wait()
+            gate = jnp.dot(xs[...], w_in[e, 0, j], preferred_element_type=jnp.float32)
+            up = jnp.dot(xs[...], w_in[e, 1, j], preferred_element_type=jnp.float32)
+            act = gate / (1.0 + jnp.exp(-gate)) * up
+            hidden[:, j * chunk : (j + 1) * chunk] = act.astype(jnp.bfloat16)
+        down_copies[e].wait()
+        if e == 0:
+            for copy in g_copies:
+                copy.wait()
+        lane = lax.broadcasted_iota(jnp.int32, gs.shape, 1) - lane_base - ids[e]
+        mine = (lane == 0) | (lane == expert_count) | (lane == 2 * expert_count)
+        scale = jnp.sum(
+            jnp.where(mine, gs[...].astype(jnp.float32), 0.0), axis=1, keepdims=True
+        )
+        for n in range(width // 512):
+            cols = slice(n * 512, (n + 1) * 512)
+            piece = scale * jnp.dot(
+                hidden[...], w_down[e, :, cols], preferred_element_type=jnp.float32
+            )
+            if e == 0:
+                total[:, cols] = piece
+            else:
+                piece = (total[:, cols] + piece).astype(jnp.bfloat16)
+                for k in range(block_count):
+                    outs[k][:, cols] = piece[k * rows : (k + 1) * rows]
+
+
+def mlp_blocks(blocks, gate_blocks, weights, ids, lane_base, expert_count, width):
+    block_count = len(blocks)
+    rows = blocks[0].shape[0]
+    half = weights[1].shape[0]
+    chunk = 256 if half % 256 == 0 else half
+    all_rows = block_count * rows
+    anywhere = pl.BlockSpec(memory_space=pl.ANY)
+    return pl.pallas_call(
+        functools.partial(
+            mlp_kernel, block_count, rows, width, half, lane_base, expert_count, chunk
+        ),
+        out_shape=[jax.ShapeDtypeStruct((rows, width), jnp.bfloat16)] * block_count,
+        in_specs=[pl.BlockSpec(memory_space=pltpu.SMEM)]
+        + [anywhere] * (2 * block_count + 4),
+        out_specs=[pl.BlockSpec(memory_space=pltpu.VMEM)] * block_count,
+        scratch_shapes=[
+            pltpu.VMEM((all_rows, width), jnp.bfloat16),
+            pltpu.VMEM((all_rows, LANES), jnp.bfloat16),
+            pltpu.VMEM((2, 2, half // chunk, width, chunk), jnp.bfloat16),
+            pltpu.VMEM((2, half, width), jnp.bfloat16),
+            pltpu.VMEM((all_rows, half), jnp.bfloat16),
+            pltpu.VMEM((all_rows, width), jnp.float32),
+            pltpu.SemaphoreType.DMA((block_count,)),
+            pltpu.SemaphoreType.DMA((block_count,)),
+            pltpu.SemaphoreType.DMA((2, 2, half // chunk)),
+            pltpu.SemaphoreType.DMA((2,)),
+        ],
+        compiler_params=pltpu.CompilerParams(vmem_limit_bytes=48 * 1024 * 1024),
+        cost_estimate=pl.CostEstimate(
+            flops=12 * all_rows * width * half,
+            bytes_accessed=12 * width * half,
+            transcendentals=2 * all_rows * half,
+        ),
+        name="expert_pair",
+    )(ids, *blocks, *gate_blocks, *weights)
+
+
+def multicast_shards(
+    ep_count,
+    chips,
+    tokens,
+    experts_one,
+    gates_one,
+    w_in_one,
+    w_down_one,
+    norm_gain,
+    experts_two,
+    gates_two,
+    placement_two,
+    w_in_two,
+    w_down_two,
+):
+    rows, width = tokens.shape
+    expert_count = placement_two.shape[0]
+    half = w_down_one.shape[1]
+    chip_count = len(chips)
+    dp_count = 2 * chip_count
+    twin = [(a, b) for pair in chips for a, b in (pair, pair[::-1])]
+
+    def along_ep(array, shift):
+        pairs = [(i, (i + shift) % ep_count) for i in range(ep_count)]
+        return lax.ppermute(array, "ep", pairs)
+
+    def along_chips(array, shift):
+        pairs = []
+        for i, pair in enumerate(chips):
+            goal = chips[(i + shift) % chip_count]
+            pairs += [(pair[0], goal[0]), (pair[1], goal[1])]
+        return lax.ppermute(array, "dp", pairs)
+
+    def across(array):
+        return lax.ppermute(array, "dp", twin)
+
+    def weights_of(w_in, w_down):
+        flat = w_in.reshape(width, 2 * half)
+        down = w_down[0]
+        return (flat, down, across(flat), across(down))
+
+    place = jnp.asarray([b for _, b in sorted(twin)], jnp.int32)
+    me = lax.axis_index("dp")
+    base = lax.axis_index("ep") * dp_count
+    ids = jnp.stack([base + me, base + place[me]]).astype(jnp.int32)
+
+    gates = jnp.concatenate(
+        [
+            gate_columns(experts_one, gates_one, expert_count),
+            gate_columns(slots_of(experts_two, placement_two), gates_two, expert_count),
+        ],
+        axis=1,
+    )
+    gates = jnp.pad(gates, ((0, 0), (0, LANES - gates.shape[1])))
+
+    def spread(block):
+        mine = [block] + [along_ep(block, k) for k in range(1, ep_count)]
+        others = [[along_chips(b, s) for b in mine] for s in range(1, chip_count)]
+        return mine, others
+
+    def gather_back(mine, others):
+        partial = []
+        for k in range(ep_count):
+            value = mine[k].astype(jnp.float32)
+            for s in range(1, chip_count):
+                value = value + along_chips(others[s - 1][k], -s).astype(jnp.float32)
+            partial.append(value)
+        total = partial[0]
+        for k in range(1, ep_count):
+            total = total + along_ep(partial[k].astype(jnp.bfloat16), -k).astype(jnp.float32)
+        return total
+
+    def layer(block, gate_blocks, weights, lane_base):
+        mine, others = spread(block)
+        if gate_blocks is None:
+            gate_blocks = [mine] + others
+        sums = [
+            mlp_blocks(bl, gb, weights, ids, lane_base, expert_count, width)
+            for bl, gb in zip([mine] + others, gate_blocks)
+        ]
+        return gather_back(sums[0], sums[1:]), gate_blocks
+
+    payload = jnp.concatenate([tokens, gates], axis=1)
+    weights_one = weights_of(w_in_one, w_down_one)
+    weights_two = weights_of(w_in_two, w_down_two)
+    moe_one, gate_blocks = layer(payload, None, weights_one, 0)
+    mixed = (tokens.astype(jnp.float32) + moe_one).astype(jnp.bfloat16)
+    mixed = lax.optimization_barrier(mixed)
+    normed = norm_rows(mixed, norm_gain)
+    moe_two, _ = layer(normed, gate_blocks, weights_two, 3 * expert_count)
+    return (mixed.astype(jnp.float32) + moe_two).astype(jnp.bfloat16)
+
+
+def chip_pairs(mesh):
+    names = mesh.axis_names
+    axes = [names.index(n) for n in ("groups", "ep", "dp", "tp")]
+    devices = mesh.devices.transpose(axes)
+    if devices.shape[3] != 1:
+        return None
+    found = None
+    for line in devices[..., 0].reshape(-1, devices.shape[2]):
+        chips = {}
+        for i, device in enumerate(line):
+            chips.setdefault(tuple(getattr(device, "coords", (i,))), []).append(i)
+        pairs = [tuple(v) for v in chips.values()]
+        if any(len(p) != 2 for p in pairs) or found not in (None, pairs):
+            return None
+        found = pairs
+    return found
 
 
 def solution(mesh):
@@ -126,4 +359,15 @@
         P(("ep", "dp"), "tp", None),
     )
     out_specs = P(("groups", "ep", "dp", "tp"), None)
-    return jax.shard_map(shards, mesh=mesh, in_specs=in_specs, out_specs=out_specs, check_vma=False)
+    chips = chip_pairs(mesh)
+
+    def run(*args):
+        experts, top_count = args[8].shape[0], args[1].shape[1]
+        body = routed_shards
+        if chips is not None and experts <= 2 * top_count and 6 * experts <= LANES:
+            body = functools.partial(multicast_shards, mesh.shape["ep"], chips)
+        return jax.shard_map(
+            body, mesh=mesh, in_specs=in_specs, out_specs=out_specs, check_vma=False
+        )(*args)
+
+    return run

time: 318 us -> 206 us (0.65); the launches traced: 317 us -> 202 us
  waiting for transfers between devices: 214 us -> 116 us
  Pallas kernels: 0 us -> 40 us
  local copies, waits for them, and re-layouts: 44.4 us -> 16 us
  matrix products: 21.1 us -> 0 us
  other arithmetic: 16.7 us -> 3.02 us
  starting transfers between devices: 21.1 us -> 25.9 us
    all_to_all x4 -> x0, waiting for transfers between devices: 214 us -> none  [the longest x2 110 us: to_owners(): lax.all_to_all(produced.reshape(expert_count, per_slot, row_width), ('ep'...]
    ppermute x0 -> x32, waiting for transfers between devices: none -> 116 us  [the longest x12 66.4 us: along_ep(): return lax.ppermute(array, 'ep', pairs)]
    pallas_call x0 -> x4, Pallas kernels: none -> 40 us  [mlp_blocks(): pl.pallas_call(functools.partial(mlp_kernel, block_count, rows, width, ha...]
    ppermute x0 -> x32, starting transfers between devices: none -> 25.9 us  [the longest x12 11.5 us: along_ep(): return lax.ppermute(array, 'ep', pairs)]
    dot_general x4 -> x0, matrix products: 21.1 us -> none  [the longest x2 13.6 us: run_expert(): jnp.dot(lax.all_gather(received, 'tp', axis=0, tiled=True), w_local, pref...]
    all_to_all x4 -> x0, starting transfers between devices: 21.1 us -> none  [the longest x2 11.3 us: to_experts(): lax.all_to_all(buffer.reshape(expert_count, per_slot, row_width), ('ep',...]
    gather x4 -> x0, local copies, waits for them, and re-layouts: 18.3 us -> none  [the longest x2 10.8 us: moe_block(): picked = returned[slot_index].reshape(tok_rows, top_count, row_width)]
    scatter x4 -> x0, local copies, waits for them, and re-layouts: 9.96 us -> none  [the longest x2 5.07 us: pack_rows(): jnp.zeros((expert_count * per_slot,), jnp.int32).at[slot_index].set(1)]
  transfers between devices with their start and end apart: 4 -> 32, of which waited for: 4 -> 19; matrix products, arithmetic and copies ran while one was open for 7% -> 4% of each run, Pallas kernels for 0% -> 15%
where the time goes in v1:
time: 206 us; the launch traced here: 202 us
  waiting for transfers between devices  116 us (56%)
  Pallas kernels  40 us (19%)
  starting transfers between devices  25.9 us (13%)
  local copies, waits for them, and re-layouts  16 us (8%)
  other arithmetic  3.02 us (1%)
    ppermute x12, waiting for transfers between devices, along_ep(): return lax.ppermute(array, 'ep', pairs)  66.4 us
    ppermute x16, waiting for transfers between devices, along_chips(): return lax.ppermute(array, 'dp', pairs)  49.9 us
    pallas_call x4, Pallas kernels, mlp_blocks(): pl.pallas_call(functools.partial(mlp_kernel, block_count, rows, width, ha...  40 us
    unnamed x36, local copies, waits for them, and re-layouts  15 us
    ppermute x12, starting transfers between devices, along_ep(): return lax.ppermute(array, 'ep', pairs)  11.5 us
    ppermute x16, starting transfers between devices, along_chips(): return lax.ppermute(array, 'dp', pairs)  10.1 us
    ppermute x4, starting transfers between devices, across(): return lax.ppermute(array, 'dp', twin)  4.24 us
  transfers between devices with their start and end apart: 32, of which 19 were waited for; matrix products, arithmetic and copies ran while one was open for 4% of the time, Pallas kernels for 15%

profile of v1, /device:TPU:11, one launch (start us, length us, event | category | flops | bytes accessed | tf_op | source)
XLA Modules:
  0.0 202.2 jit_solution(5693595893472152912)
XLA Ops:
  0.0 6.9 %copy.27 = bf16[256,8,2,768]{3,1,2,0:T(8,128)(2,1)} copy(bf16[256,8,2,768]{3,2,1,0:T(2,128)(2,1)} %bitcast.17) | data formatting | bytes 12582912
  6.9 0.7 collective-permute-start.3
  7.7 4.0 %copy.28 = bf16[256,8,2,768]{3,1,2,0:T(8,128)(2,1)} copy(bf16[256,8,2,768]{3,2,1,0:T(2,128)(2,1)S(1)} %bitcast.18) | data formatting | bytes 12582912
  11.7 0.5 collective-permute-start.19
  12.2 0.1 select_reduce_fusion.1
  12.3 0.1 copy.25
  12.7 0.1 concatenate.11
  12.8 1.0 fusion.5.refs_1_.refs_5_
  13.8 1.3 collective-permute-start
  15.1 1.1 collective-permute-start.1
  16.2 5.8 %collective-permute-done.refs_2_.refs_6_ = bf16[64,2176]{1,0:T(8,128)(2,1)S(1)} collective-permute-done((bf16[64,2176]{1,0:T(8,128)(2,1)S(1)}, bf16[64,2176]{1,0:T(8,128)(2,1)S(1)}, u32[]{:S(2)}, u32[]{:S(2)}) %collective-permute-start) | collective-permute-done | bytes 278560 | tf_op jit(solution)/shard_map/ppermute | solution.py:260
  22.0 2.1 %collective-permute-start.2 = (bf16[64,2176]{1,0:T(8,128)(2,1)S(1)}, bf16[64,2176]{1,0:T(8,128)(2,1)}, u32[]{:S(2)}, u32[]{:S(2)}) collective-permute-start(bf16[64,2176]{1,0:T(8,128)(2,1)S(1)} %fusion.5.refs_1_.refs_5_), channel_id=1, source_target_pairs={{0,12},{4,0},{8,4},{12,8},{1,13},{5,1},{9,5},{13,9},{2,14},{6,2},{... | collective-permute-start | bytes 835592 | tf_op jit(solution)/shard_map/ppermute | solution.py:260
  24.2 14.9 %collective-permute-done.1.refs_3_.refs_7_ = bf16[64,2176]{1,0:T(8,128)(2,1)} collective-permute-done((bf16[64,2176]{1,0:T(8,128)(2,1)S(1)}, bf16[64,2176]{1,0:T(8,128)(2,1)}, u32[]{:S(2)}, u32[]{:S(2)}) %collective-permute-start.1) | collective-permute-done | bytes 278560 | tf_op jit(solution)/shard_map/ppermute | solution.py:260
  39.0 0.3 collective-permute-start.5
  39.3 1.2 collective-permute-start.6
  40.5 0.7 copy-done.1
  41.2 5.1 %collective-permute-done.5.refs_1_.refs_5_ = bf16[64,2176]{1,0:T(8,128)(2,1)S(1)} collective-permute-done((bf16[64,2176]{1,0:T(8,128)(2,1)S(1)}, bf16[64,2176]{1,0:T(8,128)(2,1)S(1)}, u32[]{:S(2)}, u32[]{:S(2)}) %collective-permute-start.5) | collective-permute-done | bytes 278560 | tf_op jit(solution)/shard_map/ppermute | solution.py:267
  46.4 0.7 copy-done.3
  47.1 0.3 collective-permute-start.7
  47.3 5.0 %collective-permute-done.6.refs_2_.refs_6_ = bf16[64,2176]{1,0:T(8,128)(2,1)S(1)} collective-permute-done((bf16[64,2176]{1,0:T(8,128)(2,1)S(1)}, bf16[64,2176]{1,0:T(8,128)(2,1)S(1)}, u32[]{:S(2)}, u32[]{:S(2)}) %collective-permute-start.6) | collective-permute-done | bytes 278560 | tf_op jit(solution)/shard_map/ppermute | solution.py:267
  52.3 0.7 copy-done.5
  53.0 0.3 collective-permute-start.8
  53.3 0.6 dynamic_slice.3
  54.6 3.8 %collective-permute-done.7.refs_3_.refs_7_ = bf16[64,2176]{1,0:T(8,128)(2,1)} collective-permute-done((bf16[64,2176]{1,0:T(8,128)(2,1)}, bf16[64,2176]{1,0:T(8,128)(2,1)}, u32[]{:S(2)}, u32[]{:S(2)}) %collective-permute-start.7) | collective-permute-done | bytes 278560 | tf_op jit(solution)/shard_map/ppermute | solution.py:267
  58.4 3.1 %collective-permute-start.20 = (bf16[768,2048]{1,0:T(8,128)(2,1)}, bf16[768,2048]{1,0:T(8,128)(2,1)S(1)}, u32[]{:S(2)}, u32[]{:S(2)}) collective-permute-start(bf16[768,2048]{1,0:T(8,128)(2,1)} %bitcast.14), channel_id=1, source_target_pairs={{0,1},{1,0},{2,3},{3,2},{4,5},{5,4},{6,7},{7,6},{8,9},{9,8},{10,11... | collective-permute-start | bytes 9437192 | tf_op jit(solution)/shard_map/ppermute | solution.py:270
  61.5 2.9 %collective-permute-done.8.refs_4_.refs_8_ = bf16[64,2176]{1,0:T(8,128)(2,1)} collective-permute-done((bf16[64,2176]{1,0:T(8,128)(2,1)}, bf16[64,2176]{1,0:T(8,128)(2,1)}, u32[]{:S(2)}, u32[]{:S(2)}) %collective-permute-start.8) | collective-permute-done | bytes 278560 | tf_op jit(solution)/shard_map/ppermute | solution.py:267
  64.4 1.0 copy-done.4
  65.3 1.0 copy-done.6
  66.3 9.8 %expert_pair.5 = (bf16[64,2048]{1,0:T(8,128)(2,1)S(1)}, bf16[64,2048]{1,0:T(8,128)(2,1)S(1)}, bf16[64,2048]{1,0:T(8,128)(2,1)S(1)}, bf16[64,2048]{1,0:T(8,128)(2,1)S(1)}) custom-call(s32[2]{0:T(128)S(1)} %pad_add_fusion.refs_0_, bf16[64,2176]{1,0:T(8,128)(2,1)S(1)} %copy-done.4, bf16[64,2176]{1,0:T(8,128)(2,1)S(1)} %copy-done.6, ...), custom_call_target="tpu_custom_call" | custom-call | flops 4831838208 | bytes 18874368 | tf_op jit(solution)/shard_map/expert_pair/pallas_call | solution.py:206
  76.1 0.3 collective-permute-start.10
  76.5 1.2 collective-permute-start.12
  77.7 0.3 collective-permute-start.14
  77.9 9.8 %expert_pair.4 = (bf16[64,2048]{1,0:T(8,128)(2,1)S(1)}, bf16[64,2048]{1,0:T(8,128)(2,1)S(1)}, bf16[64,2048]{1,0:T(8,128)(2,1)S(1)}, bf16[64,2048]{1,0:T(8,128)(2,1)S(1)}) custom-call(s32[2]{0:T(128)S(1)} %pad_add_fusion.refs_0_, bf16[64,2176]{1,0:T(8,128)(2,1)S(1)} %fusion.5.refs_1_.refs_5_, bf16[64,2176]{1,0:T(8,128)(2,1)S(1)} %copy-done.2, ...), custom_call_target="tpu_custom_call" | custom-call | flops 4831838208 | bytes 18874368 | tf_op jit(solution)/shard_map/expert_pair/pallas_call | solution.py:206
  87.8 1.3 collective-permute-start.9
  89.3 4.3 %collective-permute-done.14 = bf16[64,2048]{1,0:T(8,128)(2,1)S(1)} collective-permute-done((bf16[64,2048]{1,0:T(8,128)(2,1)S(1)}, bf16[64,2048]{1,0:T(8,128)(2,1)S(1)}, u32[]{:S(2)}, u32[]{:S(2)}) %collective-permute-start.14) | collective-permute-done | bytes 262176 | tf_op jit(solution)/shard_map/ppermute | solution.py:267
  93.6 3.2 %collective-permute-start.13 = (bf16[64,2048]{1,0:T(8,128)(2,1)S(1)}, bf16[64,2048]{1,0:T(8,128)(2,1)S(1)}, u32[]{:S(2)}, u32[]{:S(2)}) collective-permute-start(bf16[64,2048]{1,0:T(8,128)(2,1)S(1)} %add_convert_fusion.5), channel_id=1, source_target_pairs={{0,8},{4,12},{8,0},{12,4},{1,9},{5,13},{9,1},{13,5},{2,10},{6,14},... | collective-permute-start | bytes 786440 | tf_op jit(solution)/shard_map/ppermute | solution.py:260
  96.8 2.3 %collective-permute-done.9 = bf16[64,2048]{1,0:T(8,128)(2,1)S(1)} collective-permute-done((bf16[64,2048]{1,0:T(8,128)(2,1)S(1)}, bf16[64,2048]{1,0:T(8,128)(2,1)S(1)}, u32[]{:S(2)}, u32[]{:S(2)}) %collective-permute-start.9) | collective-permute-done | bytes 262176 | tf_op jit(solution)/shard_map/ppermute | solution.py:267
  99.2 10.7 %collective-permute-done.13 = bf16[64,2048]{1,0:T(8,128)(2,1)S(1)} collective-permute-done((bf16[64,2048]{1,0:T(8,128)(2,1)S(1)}, bf16[64,2048]{1,0:T(8,128)(2,1)S(1)}, u32[]{:S(2)}, u32[]{:S(2)}) %collective-permute-start.13) | collective-permute-done | bytes 262176 | tf_op jit(solution)/shard_map/ppermute | solution.py:260
  109.9 5.6 %collective-permute-done.15 = bf16[64,2048]{1,0:T(8,128)(2,1)S(1)} collective-permute-done((bf16[64,2048]{1,0:T(8,128)(2,1)S(1)}, bf16[64,2048]{1,0:T(8,128)(2,1)S(1)}, u32[]{:S(2)}, u32[]{:S(2)}) %collective-permute-start.15) | collective-permute-done | bytes 262176 | tf_op jit(solution)/shard_map/ppermute | solution.py:260
  115.5 0.2 add_convert_fusion.3
  115.8 0.2 fusion.1
  115.9 0.1 fusion.3.refs_1_
  116.1 2.3 %collective-permute-start.16 = (bf16[64,2048]{1,0:T(8,128)(2,1)S(1)}, bf16[64,2048]{1,0:T(8,128)(2,1)S(1)}, u32[]{:S(2)}, u32[]{:S(2)}) collective-permute-start(bf16[64,2048]{1,0:T(8,128)(2,1)S(1)} %fusion.3.refs_1_), channel_id=1, source_target_pairs={{0,4},{4,8},{8,12},{12,0},{1,5},{5,9},{9,13},{13,1},{2,6},{6,10},{... | collective-permute-start | bytes 786440 | tf_op jit(solution)/shard_map/ppermute | solution.py:260
  118.3 1.3 collective-permute-start.18
  119.6 0.3 collective-permute-start.21
  119.9 3.5 %collective-permute-done.16.refs_2_ = bf16[64,2048]{1,0:T(8,128)(2,1)S(1)} collective-permute-done((bf16[64,2048]{1,0:T(8,128)(2,1)S(1)}, bf16[64,2048]{1,0:T(8,128)(2,1)S(1)}, u32[]{:S(2)}, u32[]{:S(2)}) %collective-permute-start.16) | collective-permute-done | bytes 262176 | tf_op jit(solution)/shard_map/ppermute | solution.py:260
  123.3 0.3 collective-permute-start.22
  123.6 16.1 %collective-permute-done.17.refs_3_ = bf16[64,2048]{1,0:T(8,128)(2,1)S(1)} collective-permute-done((bf16[64,2048]{1,0:T(8,128)(2,1)S(1)}, bf16[64,2048]{1,0:T(8,128)(2,1)S(1)}, u32[]{:S(2)}, u32[]{:S(2)}) %collective-permute-start.17) | collective-permute-done | bytes 262176 | tf_op jit(solution)/shard_map/ppermute | solution.py:260
  139.7 0.3 collective-permute-start.23
  139.9 1.2 collective-permute-start.24
  141.2 6.8 %collective-permute-done.23.refs_3_ = bf16[64,2048]{1,0:T(8,128)(2,1)S(1)} collective-permute-done((bf16[64,2048]{1,0:T(8,128)(2,1)S(1)}, bf16[64,2048]{1,0:T(8,128)(2,1)S(1)}, u32[]{:S(2)}, u32[]{:S(2)}) %collective-permute-start.23) | collective-permute-done | bytes 262176 | tf_op jit(solution)/shard_map/ppermute | solution.py:267
  148.0 5.6 %collective-permute-done.24.refs_4_ = bf16[64,2048]{1,0:T(8,128)(2,1)S(1)} collective-permute-done((bf16[64,2048]{1,0:T(8,128)(2,1)S(1)}, bf16[64,2048]{1,0:T(8,128)(2,1)S(1)}, u32[]{:S(2)}, u32[]{:S(2)}) %collective-permute-start.24) | collective-permute-done | bytes 262176 | tf_op jit(solution)/shard_map/ppermute | solution.py:267
  153.6 10.2 %expert_pair.7 = (bf16[64,2048]{1,0:T(8,128)(2,1)S(1)}, bf16[64,2048]{1,0:T(8,128)(2,1)S(1)}, bf16[64,2048]{1,0:T(8,128)(2,1)S(1)}, bf16[64,2048]{1,0:T(8,128)(2,1)S(1)}) custom-call(s32[2]{0:T(128)S(1)} %pad_add_fusion.refs_0_, bf16[64,2048]{1,0:T(8,128)(2,1)S(1)} %collective-permute-done.21.refs_1_, bf16[64,2048]{1,0:T(8,128)(2,1)S(1)} %collective-permute-done.22.refs_2_, ...), custom_call_target="tpu_custom_call" | custom-call | flops 4831838208 | bytes 18874368 | tf_op jit(solution)/shard_map/expert_pair/pallas_call | solution.py:206
  163.8 0.3 collective-permute-start.26
  164.1 10.2 %expert_pair.6 = (bf16[64,2048]{1,0:T(8,128)(2,1)S(1)}, bf16[64,2048]{1,0:T(8,128)(2,1)S(1)}, bf16[64,2048]{1,0:T(8,128)(2,1)S(1)}, bf16[64,2048]{1,0:T(8,128)(2,1)S(1)}) custom-call(s32[2]{0:T(128)S(1)} %pad_add_fusion.refs_0_, bf16[64,2048]{1,0:T(8,128)(2,1)S(1)} %fusion.3.refs_1_, bf16[64,2048]{1,0:T(8,128)(2,1)S(1)} %collective-permute-done.16.refs_2_, ...), custom_call_target="tpu_custom_call" | custom-call | flops 4831838208 | bytes 18874368 | tf_op jit(solution)/shard_map/expert_pair/pallas_call | solution.py:206
  174.3 1.3 collective-permute-start.28
  175.5 0.3 collective-permute-start.30
  175.8 1.2 collective-permute-start.25
  177.2 3.1 %collective-permute-done.28 = bf16[64,2048]{1,0:T(8,128)(2,1)S(1)} collective-permute-done((bf16[64,2048]{1,0:T(8,128)(2,1)S(1)}, bf16[64,2048]{1,0:T(8,128)(2,1)S(1)}, u32[]{:S(2)}, u32[]{:S(2)}) %collective-permute-start.28) | collective-permute-done | bytes 262176 | tf_op jit(solution)/shard_map/ppermute | solution.py:267
  180.4 5.5 %collective-permute-done.30 = bf16[64,2048]{1,0:T(8,128)(2,1)S(1)} collective-permute-done((bf16[64,2048]{1,0:T(8,128)(2,1)S(1)}, bf16[64,2048]{1,0:T(8,128)(2,1)S(1)}, u32[]{:S(2)}, u32[]{:S(2)}) %collective-permute-start.30) | collective-permute-done | bytes 262176 | tf_op jit(solution)/shard_map/ppermute | solution.py:267
  186.0 5.5 %collective-permute-done.25 = bf16[64,2048]{1,0:T(8,128)(2,1)S(1)} collective-permute-done((bf16[64,2048]{1,0:T(8,128)(2,1)S(1)}, bf16[64,2048]{1,0:T(8,128)(2,1)S(1)}, u32[]{:S(2)}, u32[]{:S(2)}) %collective-permute-start.25) | collective-permute-done | bytes 262176 | tf_op jit(solution)/shard_map/ppermute | solution.py:267
  191.4 4.2 %collective-permute-done.29 = bf16[64,2048]{1,0:T(8,128)(2,1)S(1)} collective-permute-done((bf16[64,2048]{1,0:T(8,128)(2,1)S(1)}, bf16[64,2048]{1,0:T(8,128)(2,1)S(1)}, u32[]{:S(2)}, u32[]{:S(2)}) %collective-permute-start.29) | collective-permute-done | bytes 262176 | tf_op jit(solution)/shard_map/ppermute | solution.py:260
  195.7 5.6 %collective-permute-done.31 = bf16[64,2048]{1,0:T(8,128)(2,1)S(1)} collective-permute-done((bf16[64,2048]{1,0:T(8,128)(2,1)S(1)}, bf16[64,2048]{1,0:T(8,128)(2,1)S(1)}, u32[]{:S(2)}, u32[]{:S(2)}) %collective-permute-start.31) | collective-permute-done | bytes 262176 | tf_op jit(solution)/shard_map/ppermute | solution.py:260
  201.3 0.9 fusion.4
  (65 shorter events, 1.1 us)
Async XLA Ops:
  0.0 7.6 %copy-start = (bf16[1,768,2048]{2,1,0:T(8,128)(2,1)S(1)}, bf16[1,768,2048]{2,1,0:T(8,128)(2,1)}, u32[]{:S(2)}) copy-start(bf16[1,768,2048]{2,1,0:T(8,128)(2,1)} %param.16) | copy-start | bytes 9437188
  0.0 7.6 %copy-start.8 = (bf16[1,2048,2,768]{3,2,1,0:T(2,128)(2,1)S(1)}, bf16[1,2048,2,768]{3,2,1,0:T(2,128)(2,1)}, u32[]{:S(2)}) copy-start(bf16[1,2048,2,768]{3,2,1,0:T(2,128)(2,1)} %param.21) | copy-start | bytes 18874372
  6.9 57.5 %collective-permute-start.3 = (bf16[2048,1536]{1,0:T(8,128)(2,1)}, bf16[2048,1536]{1,0:T(8,128)(2,1)}, u32[]{:S(2)}, u32[]{:S(2)}) collective-permute-start(bf16[2048,1536]{1,0:T(8,128)(2,1)} %bitcast.7.refs_9_), channel_id=1, source_target_pairs={{0,1},{1,0},{2,3},{3,2},{4,5},{5,4},{6,7},{7,6},{8,9},{9,8},{10,11... | collective-permute-start | bytes 18874376 | tf_op jit(solution)/shard_map/ppermute | solution.py:270
  7.6 56.8 %collective-permute-start.4 = (bf16[768,2048]{1,0:T(8,128)(2,1)S(1)}, bf16[768,2048]{1,0:T(8,128)(2,1)}, u32[]{:S(2)}, u32[]{:S(2)}) collective-permute-start(bf16[768,2048]{1,0:T(8,128)(2,1)S(1)} %bitcast.11), channel_id=1, source_target_pairs={{0,1},{1,0},{2,3},{3,2},{4,5},{5,4},{6,7},{7,6},{8,9},{9,8},{10,11... | collective-permute-start | bytes 9437192 | tf_op jit(solution)/shard_map/ppermute | solution.py:270
  7.6 4.6 %copy-start.11 = (s32[64,8]{0,1:T(8,128)S(1)}, s32[64,8]{0,1:T(8,128)}, u32[]{:S(2)}) copy-start(s32[64,8]{0,1:T(8,128)} %param.18) | copy-start | bytes 6148
  7.6 4.5 %copy-start.15 = (s32[16]{0:T(128)S(1)}, s32[16]{0:T(128)}, u32[]{:S(2)}) copy-start(s32[16]{0:T(128)} %param.20) | copy-start | bytes 196
  7.6 4.6 %copy-start.12 = (f32[64,8]{0,1:T(8,128)S(1)}, f32[64,8]{0,1:T(8,128)}, u32[]{:S(2)}) copy-start(f32[64,8]{0,1:T(8,128)} %param.19) | copy-start | bytes 6148
  7.6 4.7 %copy-start.13 = (f32[64,8]{0,1:T(8,128)S(1)}, f32[64,8]{0,1:T(8,128)}, u32[]{:S(2)}) copy-start(f32[64,8]{0,1:T(8,128)} %param.14) | copy-start | bytes 6148
  7.7 4.7 %copy-start.14 = (s32[64,8]{0,1:T(8,128)S(1)}, s32[64,8]{0,1:T(8,128)}, u32[]{:S(2)}) copy-start(s32[64,8]{0,1:T(8,128)} %param.13) | copy-start | bytes 6148
  7.7 45.6 %copy-start.16 = (s32[4]{0:T(128)S(1)}, s32[4]{0:T(128)}, u32[]{:S(2)}) copy-start(s32[4]{0:T(128)} %constant.22.clone) | copy-start | bytes 52
  11.7 129.5 %collective-permute-start.19 = (bf16[2048,1536]{1,0:T(8,128)(2,1)}, bf16[2048,1536]{1,0:T(8,128)(2,1)}, u32[]{:S(2)}, u32[]{:S(2)}) collective-permute-start(bf16[2048,1536]{1,0:T(8,128)(2,1)} %bitcast.10.refs_9_), channel_id=1, source_target_pairs={{0,1},{1,0},{2,3},{3,2},{4,5},{5,4},{6,7},{7,6},{8,9},{9,8},{10,11... | collective-permute-start | bytes 18874376 | tf_op jit(solution)/shard_map/ppermute | solution.py:270
  13.8 8.2 %collective-permute-start = (bf16[64,2176]{1,0:T(8,128)(2,1)S(1)}, bf16[64,2176]{1,0:T(8,128)(2,1)S(1)}, u32[]{:S(2)}, u32[]{:S(2)}) collective-permute-start(bf16[64,2176]{1,0:T(8,128)(2,1)S(1)} %fusion.5.refs_1_.refs_5_), channel_id=1, source_target_pairs={{0,4},{4,8},{8,12},{12,0},{1,5},{5,9},{9,13},{13,1},{2,6},{6,10},{... | collective-permute-start | bytes 835592 | tf_op jit(solution)/shard_map/ppermute | solution.py:260
  15.1 23.9 %collective-permute-start.1 = (bf16[64,2176]{1,0:T(8,128)(2,1)S(1)}, bf16[64,2176]{1,0:T(8,128)(2,1)}, u32[]{:S(2)}, u32[]{:S(2)}) collective-permute-start(bf16[64,2176]{1,0:T(8,128)(2,1)S(1)} %fusion.5.refs_1_.refs_5_), channel_id=1, source_target_pairs={{0,8},{4,12},{8,0},{12,4},{1,9},{5,13},{9,1},{13,5},{2,10},{6,14},... | collective-permute-start | bytes 835592 | tf_op jit(solution)/shard_map/ppermute | solution.py:260
  22.0 17.3 %collective-permute-start.2 = (bf16[64,2176]{1,0:T(8,128)(2,1)S(1)}, bf16[64,2176]{1,0:T(8,128)(2,1)}, u32[]{:S(2)}, u32[]{:S(2)}) collective-permute-start(bf16[64,2176]{1,0:T(8,128)(2,1)S(1)} %fusion.5.refs_1_.refs_5_), channel_id=1, source_target_pairs={{0,12},{4,0},{8,4},{12,8},{1,13},{5,1},{9,5},{13,9},{2,14},{6,2},{... | collective-permute-start | bytes 835592 | tf_op jit(solution)/shard_map/ppermute | solution.py:260
  39.0 7.3 %collective-permute-start.5 = (bf16[64,2176]{1,0:T(8,128)(2,1)S(1)}, bf16[64,2176]{1,0:T(8,128)(2,1)S(1)}, u32[]{:S(2)}, u32[]{:S(2)}) collective-permute-start(bf16[64,2176]{1,0:T(8,128)(2,1)S(1)} %fusion.5.refs_1_.refs_5_), channel_id=1, source_target_pairs={{0,2},{1,3},{2,0},{3,1},{4,6},{5,7},{6,4},{7,5},{8,10},{9,11},{10,... | collective-permute-start | bytes 835592 | tf_op jit(solution)/shard_map/ppermute | solution.py:267
  39.3 13.0 %collective-permute-start.6 = (bf16[64,2176]{1,0:T(8,128)(2,1)S(1)}, bf16[64,2176]{1,0:T(8,128)(2,1)S(1)}, u32[]{:S(2)}, u32[]{:S(2)}) collective-permute-start(bf16[64,2176]{1,0:T(8,128)(2,1)S(1)} %collective-permute-done.refs_2_.refs_6_), channel_id=1, source_target_pairs={{0,2},{1,3},{2,0},{3,1},{4,6},{5,7},{6,4},{7,5},{8,10},{9,11},{10,... | collective-permute-start | bytes 835592 | tf_op jit(solution)/shard_map/ppermute | solution.py:267
  40.5 0.7 copy-start.1
  46.4 0.7 copy-start.3
  47.1 11.3 %collective-permute-start.7 = (bf16[64,2176]{1,0:T(8,128)(2,1)}, bf16[64,2176]{1,0:T(8,128)(2,1)}, u32[]{:S(2)}, u32[]{:S(2)}) collective-permute-start(bf16[64,2176]{1,0:T(8,128)(2,1)} %collective-permute-done.1.refs_3_.refs_7_), channel_id=1, source_target_pairs={{0,2},{1,3},{2,0},{3,1},{4,6},{5,7},{6,4},{7,5},{8,10},{9,11},{10,... | collective-permute-start | bytes 835592 | tf_op jit(solution)/shard_map/ppermute | solution.py:267
  52.3 0.7 copy-start.5
  53.0 11.3 %collective-permute-start.8 = (bf16[64,2176]{1,0:T(8,128)(2,1)}, bf16[64,2176]{1,0:T(8,128)(2,1)}, u32[]{:S(2)}, u32[]{:S(2)}) collective-permute-start(bf16[64,2176]{1,0:T(8,128)(2,1)} %collective-permute-done.2.refs_4_.refs_8_), channel_id=1, source_target_pairs={{0,2},{1,3},{2,0},{3,1},{4,6},{5,7},{6,4},{7,5},{8,10},{9,11},{10,... | collective-permute-start | bytes 835592 | tf_op jit(solution)/shard_map/ppermute | solution.py:267
  58.4 19.5 %copy-start.2 = (bf16[64,2176]{1,0:T(8,128)(2,1)S(1)}, bf16[64,2176]{1,0:T(8,128)(2,1)}, u32[]{:S(2)}) copy-start(bf16[64,2176]{1,0:T(8,128)(2,1)} %copy-done.1) | copy-start | bytes 835588
  58.4 61.2 %collective-permute-start.20 = (bf16[768,2048]{1,0:T(8,128)(2,1)}, bf16[768,2048]{1,0:T(8,128)(2,1)S(1)}, u32[]{:S(2)}, u32[]{:S(2)}) collective-permute-start(bf16[768,2048]{1,0:T(8,128)(2,1)} %bitcast.14), channel_id=1, source_target_pairs={{0,1},{1,0},{2,3},{3,2},{4,5},{5,4},{6,7},{7,6},{8,9},{9,8},{10,11... | collective-permute-start | bytes 9437192 | tf_op jit(solution)/shard_map/ppermute | solution.py:270
  64.4 1.0 copy-start.4
  65.3 1.0 copy-start.6
  76.1 11.6 %collective-permute-start.10 = (bf16[64,2048]{1,0:T(8,128)(2,1)S(1)}, bf16[64,2048]{1,0:T(8,128)(2,1)S(1)}, u32[]{:S(2)}, u32[]{:S(2)}) collective-permute-start(bf16[64,2048]{1,0:T(8,128)(2,1)S(1)} %get-tuple-element.24), channel_id=1, source_target_pairs={{0,2},{1,3},{2,0},{3,1},{4,6},{5,7},{6,4},{7,5},{8,10},{9,11},{10,... | collective-permute-start | bytes 786440 | tf_op jit(solution)/shard_map/ppermute | solution.py:267
  76.5 12.7 %collective-permute-start.12 = (bf16[64,2048]{1,0:T(8,128)(2,1)S(1)}, bf16[64,2048]{1,0:T(8,128)(2,1)S(1)}, u32[]{:S(2)}, u32[]{:S(2)}) collective-permute-start(bf16[64,2048]{1,0:T(8,128)(2,1)S(1)} %get-tuple-element.26), channel_id=1, source_target_pairs={{0,2},{1,3},{2,0},{3,1},{4,6},{5,7},{6,4},{7,5},{8,10},{9,11},{10,... | collective-permute-start | bytes 786440 | tf_op jit(solution)/shard_map/ppermute | solution.py:267
  77.7 37.9 %copy-start.9 = (bf16[64,2048]{1,0:T(8,128)(2,1)S(1)}, bf16[64,2048]{1,0:T(8,128)(2,1)}, u32[]{:S(2)}) copy-start(bf16[64,2048]{1,0:T(8,128)(2,1)} %param.12) | copy-start | bytes 786436
  77.7 38.3 %copy-start.10 = (f32[2048]{0:T(1024)S(1)}, f32[2048]{0:T(1024)}, u32[]{:S(2)}) copy-start(f32[2048]{0:T(1024)} %param.17) | copy-start | bytes 24580
  77.7 15.9 %collective-permute-start.14 = (bf16[64,2048]{1,0:T(8,128)(2,1)S(1)}, bf16[64,2048]{1,0:T(8,128)(2,1)S(1)}, u32[]{:S(2)}, u32[]{:S(2)}) collective-permute-start(bf16[64,2048]{1,0:T(8,128)(2,1)S(1)} %get-tuple-element.28), channel_id=1, source_target_pairs={{0,2},{1,3},{2,0},{3,1},{4,6},{5,7},{6,4},{7,5},{8,10},{9,11},{10,... | collective-permute-start | bytes 786440 | tf_op jit(solution)/shard_map/ppermute | solution.py:267
  87.8 11.4 %collective-permute-start.9 = (bf16[64,2048]{1,0:T(8,128)(2,1)S(1)}, bf16[64,2048]{1,0:T(8,128)(2,1)S(1)}, u32[]{:S(2)}, u32[]{:S(2)}) collective-permute-start(bf16[64,2048]{1,0:T(8,128)(2,1)S(1)} %get-tuple-element.22), channel_id=1, source_target_pairs={{0,2},{1,3},{2,0},{3,1},{4,6},{5,7},{6,4},{7,5},{8,10},{9,11},{10,... | collective-permute-start | bytes 786440 | tf_op jit(solution)/shard_map/ppermute | solution.py:267
  89.1 10.0 %collective-permute-start.11 = (bf16[64,2048]{1,0:T(8,128)(2,1)S(1)}, bf16[64,2048]{1,0:T(8,128)(2,1)S(1)}, u32[]{:S(2)}, u32[]{:S(2)}) collective-permute-start(bf16[64,2048]{1,0:T(8,128)(2,1)S(1)} %add_convert_fusion.6), channel_id=1, source_target_pairs={{0,12},{4,0},{8,4},{12,8},{1,13},{5,1},{9,5},{13,9},{2,14},{6,2},{... | collective-permute-start | bytes 786440 | tf_op jit(solution)/shard_map/ppermute | solution.py:260
  93.6 16.4 %collective-permute-start.13 = (bf16[64,2048]{1,0:T(8,128)(2,1)S(1)}, bf16[64,2048]{1,0:T(8,128)(2,1)S(1)}, u32[]{:S(2)}, u32[]{:S(2)}) collective-permute-start(bf16[64,2048]{1,0:T(8,128)(2,1)S(1)} %add_convert_fusion.5), channel_id=1, source_target_pairs={{0,8},{4,12},{8,0},{12,4},{1,9},{5,13},{9,1},{13,5},{2,10},{6,14},... | collective-permute-start | bytes 786440 | tf_op jit(solution)/shard_map/ppermute | solution.py:260
  99.2 16.4 %collective-permute-start.15 = (bf16[64,2048]{1,0:T(8,128)(2,1)S(1)}, bf16[64,2048]{1,0:T(8,128)(2,1)S(1)}, u32[]{:S(2)}, u32[]{:S(2)}) collective-permute-start(bf16[64,2048]{1,0:T(8,128)(2,1)S(1)} %add_convert_fusion.4), channel_id=1, source_target_pairs={{0,4},{4,8},{8,12},{12,0},{1,5},{5,9},{9,13},{13,1},{2,6},{6,10},{... | collective-permute-start | bytes 786440 | tf_op jit(solution)/shard_map/ppermute | solution.py:260
  116.1 7.3 %collective-permute-start.16 = (bf16[64,2048]{1,0:T(8,128)(2,1)S(1)}, bf16[64,2048]{1,0:T(8,128)(2,1)S(1)}, u32[]{:S(2)}, u32[]{:S(2)}) collective-permute-start(bf16[64,2048]{1,0:T(8,128)(2,1)S(1)} %fusion.3.refs_1_), channel_id=1, source_target_pairs={{0,4},{4,8},{8,12},{12,0},{1,5},{5,9},{9,13},{13,1},{2,6},{6,10},{... | collective-permute-start | bytes 786440 | tf_op jit(solution)/shard_map/ppermute | solution.py:260
  118.3 21.3 %collective-permute-start.17 = (bf16[64,2048]{1,0:T(8,128)(2,1)S(1)}, bf16[64,2048]{1,0:T(8,128)(2,1)S(1)}, u32[]{:S(2)}, u32[]{:S(2)}) collective-permute-start(bf16[64,2048]{1,0:T(8,128)(2,1)S(1)} %fusion.3.refs_1_), channel_id=1, source_target_pairs={{0,8},{4,12},{8,0},{12,4},{1,9},{5,13},{9,1},{13,5},{2,10},{6,14},... | collective-permute-start | bytes 786440 | tf_op jit(solution)/shard_map/ppermute | solution.py:260
  118.3 21.6 %collective-permute-start.18 = (bf16[64,2048]{1,0:T(8,128)(2,1)S(1)}, bf16[64,2048]{1,0:T(8,128)(2,1)S(1)}, u32[]{:S(2)}, u32[]{:S(2)}) collective-permute-start(bf16[64,2048]{1,0:T(8,128)(2,1)S(1)} %fusion.3.refs_1_), channel_id=1, source_target_pairs={{0,12},{4,0},{8,4},{12,8},{1,13},{5,1},{9,5},{13,9},{2,14},{6,2},{... | collective-permute-start | bytes 786440 | tf_op jit(solution)/shard_map/ppermute | solution.py:260
  119.6 34.0 %copy-start.7 = (bf16[768,2048]{1,0:T(8,128)(2,1)}, bf16[768,2048]{1,0:T(8,128)(2,1)S(1)}, u32[]{:S(2)}) copy-start(bf16[768,2048]{1,0:T(8,128)(2,1)S(1)} %collective-permute-done.20.refs_12_) | copy-start | bytes 9437188
  119.6 21.6 %collective-permute-start.21 = (bf16[64,2048]{1,0:T(8,128)(2,1)S(1)}, bf16[64,2048]{1,0:T(8,128)(2,1)S(1)}, u32[]{:S(2)}, u32[]{:S(2)}) collective-permute-start(bf16[64,2048]{1,0:T(8,128)(2,1)S(1)} %fusion.3.refs_1_), channel_id=1, source_target_pairs={{0,2},{1,3},{2,0},{3,1},{4,6},{5,7},{6,4},{7,5},{8,10},{9,11},{10,... | collective-permute-start | bytes 786440 | tf_op jit(solution)/shard_map/ppermute | solution.py:267
  123.3 17.8 %collective-permute-start.22 = (bf16[64,2048]{1,0:T(8,128)(2,1)S(1)}, bf16[64,2048]{1,0:T(8,128)(2,1)S(1)}, u32[]{:S(2)}, u32[]{:S(2)}) collective-permute-start(bf16[64,2048]{1,0:T(8,128)(2,1)S(1)} %collective-permute-done.16.refs_2_), channel_id=1, source_target_pairs={{0,2},{1,3},{2,0},{3,1},{4,6},{5,7},{6,4},{7,5},{8,10},{9,11},{10,... | collective-permute-start | bytes 786440 | tf_op jit(solution)/shard_map/ppermute | solution.py:267
  139.7 8.3 %collective-permute-start.23 = (bf16[64,2048]{1,0:T(8,128)(2,1)S(1)}, bf16[64,2048]{1,0:T(8,128)(2,1)S(1)}, u32[]{:S(2)}, u32[]{:S(2)}) collective-permute-start(bf16[64,2048]{1,0:T(8,128)(2,1)S(1)} %collective-permute-done.17.refs_3_), channel_id=1, source_target_pairs={{0,2},{1,3},{2,0},{3,1},{4,6},{5,7},{6,4},{7,5},{8,10},{9,11},{10,... | collective-permute-start | bytes 786440 | tf_op jit(solution)/shard_map/ppermute | solution.py:267
  139.9 13.7 %collective-permute-start.24 = (bf16[64,2048]{1,0:T(8,128)(2,1)S(1)}, bf16[64,2048]{1,0:T(8,128)(2,1)S(1)}, u32[]{:S(2)}, u32[]{:S(2)}) collective-permute-start(bf16[64,2048]{1,0:T(8,128)(2,1)S(1)} %collective-permute-done.18.refs_4_), channel_id=1, source_target_pairs={{0,2},{1,3},{2,0},{3,1},{4,6},{5,7},{6,4},{7,5},{8,10},{9,11},{10,... | collective-permute-start | bytes 786440 | tf_op jit(solution)/shard_map/ppermute | solution.py:267
  163.8 13.2 %collective-permute-start.26 = (bf16[64,2048]{1,0:T(8,128)(2,1)S(1)}, bf16[64,2048]{1,0:T(8,128)(2,1)S(1)}, u32[]{:S(2)}, u32[]{:S(2)}) collective-permute-start(bf16[64,2048]{1,0:T(8,128)(2,1)S(1)} %get-tuple-element.32), channel_id=1, source_target_pairs={{0,2},{1,3},{2,0},{3,1},{4,6},{5,7},{6,4},{7,5},{8,10},{9,11},{10,... | collective-permute-start | bytes 786440 | tf_op jit(solution)/shard_map/ppermute | solution.py:267
  174.3 5.9 %collective-permute-start.28 = (bf16[64,2048]{1,0:T(8,128)(2,1)S(1)}, bf16[64,2048]{1,0:T(8,128)(2,1)S(1)}, u32[]{:S(2)}, u32[]{:S(2)}) collective-permute-start(bf16[64,2048]{1,0:T(8,128)(2,1)S(1)} %get-tuple-element.34), channel_id=1, source_target_pairs={{0,2},{1,3},{2,0},{3,1},{4,6},{5,7},{6,4},{7,5},{8,10},{9,11},{10,... | collective-permute-start | bytes 786440 | tf_op jit(solution)/shard_map/ppermute | solution.py:267
  175.5 10.3 %collective-permute-start.30 = (bf16[64,2048]{1,0:T(8,128)(2,1)S(1)}, bf16[64,2048]{1,0:T(8,128)(2,1)S(1)}, u32[]{:S(2)}, u32[]{:S(2)}) collective-permute-start(bf16[64,2048]{1,0:T(8,128)(2,1)S(1)} %get-tuple-element.36), channel_id=1, source_target_pairs={{0,2},{1,3},{2,0},{3,1},{4,6},{5,7},{6,4},{7,5},{8,10},{9,11},{10,... | collective-permute-start | bytes 786440 | tf_op jit(solution)/shard_map/ppermute | solution.py:267
  175.8 15.6 %collective-permute-start.25 = (bf16[64,2048]{1,0:T(8,128)(2,1)S(1)}, bf16[64,2048]{1,0:T(8,128)(2,1)S(1)}, u32[]{:S(2)}, u32[]{:S(2)}) collective-permute-start(bf16[64,2048]{1,0:T(8,128)(2,1)S(1)} %get-tuple-element.30), channel_id=1, source_target_pairs={{0,2},{1,3},{2,0},{3,1},{4,6},{5,7},{6,4},{7,5},{8,10},{9,11},{10,... | collective-permute-start | bytes 786440 | tf_op jit(solution)/shard_map/ppermute | solution.py:267
  177.1 14.4 %collective-permute-start.27 = (bf16[64,2048]{1,0:T(8,128)(2,1)S(1)}, bf16[64,2048]{1,0:T(8,128)(2,1)S(1)}, u32[]{:S(2)}, u32[]{:S(2)}) collective-permute-start(bf16[64,2048]{1,0:T(8,128)(2,1)S(1)} %add_convert_fusion.2), channel_id=1, source_target_pairs={{0,12},{4,0},{8,4},{12,8},{1,13},{5,1},{9,5},{13,9},{2,14},{6,2},{... | collective-permute-start | bytes 786440 | tf_op jit(solution)/shard_map/ppermute | solution.py:260
  180.3 15.4 %collective-permute-start.29 = (bf16[64,2048]{1,0:T(8,128)(2,1)S(1)}, bf16[64,2048]{1,0:T(8,128)(2,1)S(1)}, u32[]{:S(2)}, u32[]{:S(2)}) collective-permute-start(bf16[64,2048]{1,0:T(8,128)(2,1)S(1)} %add_convert_fusion.1), channel_id=1, source_target_pairs={{0,8},{4,12},{8,0},{12,4},{1,9},{5,13},{9,1},{13,5},{2,10},{6,14},... | collective-permute-start | bytes 786440 | tf_op jit(solution)/shard_map/ppermute | solution.py:260
  185.9 15.4 %collective-permute-start.31 = (bf16[64,2048]{1,0:T(8,128)(2,1)S(1)}, bf16[64,2048]{1,0:T(8,128)(2,1)S(1)}, u32[]{:S(2)}, u32[]{:S(2)}) collective-permute-start(bf16[64,2048]{1,0:T(8,128)(2,1)S(1)} %add_convert_fusion), channel_id=1, source_target_pairs={{0,4},{4,8},{8,12},{12,0},{1,5},{5,9},{9,13},{13,1},{2,6},{6,10},{... | collective-permute-start | bytes 786440 | tf_op jit(solution)/shard_map/ppermute | solution.py:260
